TPU v7x, 32 devices: a whole 2x2x4 slice. The times are simulated.
32 devices in a mesh: elem: 16 (over z, y, core), test: 2 (over x).
Axes of the slice: x: 2, y: 2, z: 4, core: 2. Of those that a mesh axis runs over, the one named last changes fastest.
Arguments:
- mode_fields: bfloat16 [64, 3, 65536], P('test', None, 'elem'), may hold values from -6 to 6
- elem_type: int32 [128], P('elem'), may hold values from 0 to 3
- type_scales: float32 [4, 3], replicated, may hold values from 0.5 to 2
Outputs:
- conv_tensor: float32 [64, 64, 64], P('test', 'elem')
All inputs are finite; a program needn't handle non-finite values.
Results may differ from a plain program's by a relative error of at most 0.0051.
Values may be sent and summed in bfloat16 or wider, within the bound.
A program may use at most 64 MiB of HBM per device.

v0:
```python
import jax
import jax.numpy as jnp
import numpy as np
from jax import lax
from jax.sharding import PartitionSpec as P

Q = 8
block_modes = 4


def legendre_top(points, degree):
    before = points * 0.0 + 1.0
    current = points
    for order in range(2, degree + 1):
        following = ((2 * order - 1) * points * current - (order - 1) * before) / order
        before = current
        current = following
    return (current, before)


def lobatto_tables(order_points):
    degree = order_points - 1
    lobatto_nodes = np.cos(np.pi * np.arange(degree + 1) / degree)
    for sweep in range(100):
        top, lower = legendre_top(lobatto_nodes, degree)
        lobatto_nodes = lobatto_nodes - (lobatto_nodes * top - lower) / ((degree + 1) * top)
    lobatto_nodes = lobatto_nodes[::-1].copy()
    lobatto_nodes[0] = -1.0
    lobatto_nodes[-1] = 1.0
    values, unused = legendre_top(lobatto_nodes, degree)
    weights = 2.0 / (degree * (degree + 1) * values**2)
    identity = np.eye(order_points)
    distance = lobatto_nodes[:, None] - lobatto_nodes[None, :]
    spacing = np.where(identity > 0, 1.0, distance)
    derivative = np.where(identity > 0, 0.0, values[:, None] / values[None, :] / spacing)
    corner = degree * (degree + 1) / 4.0
    ends = np.concatenate([[-corner], np.zeros(degree - 1), [corner]])
    derivative = derivative + identity * ends[None, :]
    square_eye = np.eye(order_points * order_points)
    along_r = np.kron(square_eye, derivative)
    along_s = np.kron(identity, np.kron(derivative, identity))
    along_t = np.kron(derivative, square_eye)
    table = np.concatenate([along_r.T, along_s.T, along_t.T], axis=1)
    cube_weights = np.kron(weights, np.kron(weights, weights))
    return (table.astype(np.float32), cube_weights.astype(np.float32))


def element_scales(types, type_scales):
    picks = (types[:, None] == jnp.arange(type_scales.shape[0], dtype=jnp.int32)[None, :]).astype(
        jnp.float32
    )
    return jnp.sum(picks[:, :, None] * type_scales[None, :, :], axis=1)


def gradient(fields, scales, table, cube):
    mode_count = fields.shape[0]
    elements = fields.shape[2] // cube
    flat = fields.reshape(mode_count * 3 * elements, cube)
    derived = jnp.dot(flat, table, preferred_element_type=jnp.float32).reshape(
        mode_count, 3, elements, 3, cube
    )
    return (derived * scales[None, None, :, :, None]).astype(jnp.bfloat16)


def project(test_fields, trial_fields, grads, quadrature):
    test_modes = test_fields.shape[0]
    trial_modes = trial_fields.shape[0]
    grad_modes = grads.shape[0]
    blocks = grads.reshape((grad_modes // block_modes, block_modes) + grads.shape[1:])
    test_wide = test_fields.astype(jnp.float32)

    def one_block(grad_block):
        grad_wide = grad_block.astype(jnp.float32)
        summed = test_wide[:, None, 0, :, None, :] * grad_wide[None, :, 0]
        summed = summed + test_wide[:, None, 1, :, None, :] * grad_wide[None, :, 1]
        summed = summed + test_wide[:, None, 2, :, None, :] * grad_wide[None, :, 2]
        pairs = (summed * quadrature[None, None, :, None, :]).astype(jnp.bfloat16)
        return jnp.einsum(
            "ikedp,jdep->ijk", pairs, trial_fields, preferred_element_type=jnp.float32
        )

    result = lax.map(one_block, blocks)
    return result.transpose(1, 2, 0, 3).reshape(test_modes, trial_modes, grad_modes)


def body(mode_fields, elem_type, type_scales):
    table, cube_weights = lobatto_tables(Q)
    table = jnp.asarray(table).astype(jnp.bfloat16)
    point_weights = jnp.asarray(cube_weights).astype(jnp.float32)
    cube = Q**3
    total_points = mode_fields.shape[2] * lax.axis_size("elem")
    gathered = lax.all_gather(mode_fields, "test", axis=0, tiled=True)
    elements = mode_fields.shape[2] // cube
    scales = element_scales(elem_type, type_scales)
    quadrature = point_weights[None, :] / jnp.prod(scales, axis=1)[:, None]
    grads = gradient(gathered, scales, table, cube)
    partial_value = project(
        mode_fields.reshape(mode_fields.shape[0], 3, elements, cube),
        gathered.reshape(gathered.shape[0], 3, elements, cube),
        grads,
        quadrature,
    )
    summed = lax.psum_scatter(partial_value, "elem", scatter_dimension=1, tiled=True)
    return summed * float(total_points) ** (-0.5)


def solution(mesh):
    placed = (P("test", None, "elem"), P("elem"), P())
    return jax.shard_map(
        body, mesh=mesh, in_specs=placed, out_specs=P("test", "elem", None), check_vma=False
    )
```

profile of v0, /device:TPU:0, one launch (start us, length us, event | category | flops | bytes accessed | tf_op | source)
XLA Modules:
  0.0 182.2 jit_solution(7041535098381613878)
XLA Ops:
  6.5 0.7 all-gather.2.cloned.1.call-update
  7.3 1.3 convert_element_type.34
  8.6 0.8 copy.20
  9.7 29.2 %all-gather.2.cloned.1.call-done = bf16[64,3,4096]{2,0,1:T(8,128)(2,1)} async-done(((bf16[32,3,4096]{2,0,1:T(8,128)(2,1)}), bf16[64,3,4096]{2,0,1:T(8,128)(2,1)}) %all-gather.2.cloned.1.call-update) | async-done | bytes 1572880 | tf_op jit(solution)/shard_map/all_gather | solution.py:92
  38.8 1.6 copy.40
  40.4 6.7 %fusion.11 = bf16[64,3,8,3,512]{4,0,2,1,3:T(8,128)(2,1)} fusion(f32[8,3]{0,1:T(4,128)S(1)} %multiply_reduce_fusion, bf16[3,512,512,1,1]{2,1,4,3,0:T(8,128)(2,1)} %constant.28, bf16[3,8,8,8,512]{4,3,2,1,0:T(8,128)(2,1)} %bitcast.79), kind=kOutput, calls=%fused_computation.17 | convolution fusion | flops 2420637696 | bytes 7864416 | tf_op jit(solution)/shard_map/dot_general | solution.py:59
  47.2 7.7 %reshape.50 = bf16[16,4,3,8,3,512]{5,1,0,3,2,4:T(4,128)(2,1)} reshape(bf16[64,3,8,3,512]{4,0,2,1,3:T(8,128)(2,1)} %fusion.11) | data formatting | bytes 9437184 | tf_op jit(solution)/shard_map/reshape | solution.py:69
  54.9 58.1 %while.11 = (s32[]{:T(128)}, f32[16,32,64,4]{2,1,3,0:T(8,128)}, f32[32,3,8,512]{3,0,2,1:T(8,128)S(1)}, bf16[16,4,3,8,3,512]{5,1,0,3,2,4:T(4,128)(2,1)}, bf16[64,...) while((s32[]{:T(128)}, f32[16,32,64,4]{2,1,3,0:T(8,128)}, ...), condition=%wide.region_3.4_spmd.clone, body=%wide.region_2.3_spmd.clone.sunk | while | flops 212488192 | bytes 9636473 | solution.py:82
  54.9 1.1 constant_dynamic-slice_fusion.2
  56.1 0.2 slice_bitcast_fusion.9
  56.3 2.1 %fusion.20 = f32[16,32,64,4]{2,1,3,0:T(8,128)} fusion(f32[16,32,64,4]{2,1,3,0:T(8,128)} %get-tuple-element.168, s32[]{:T(128)} %get-tuple-element.167, bf16[64,3,8,512]{3,0,2,1:T(8,128)(2,1)S(1)} %get-tuple-element.179, f32[8,512]{1,0:T(8,128)S(1)} %broadcast_divide_fusion.2, f32[4,8,3,512]{3,1,0,2:T(8,128)S(1)} %get-tuple-element.153, ...), kind=kOutput, calls=%fused_computation.5.clone.1 | convolution fusion | flops 212336640 | bytes 3817984 | tf_op jit(solution)/shard_map/while/body/eval_jaxpr/ikedp,jdep->ijk/dot_general | solution.py:78
  58.5 1.1 constant_dynamic-slice_fusion.2
  59.7 0.2 slice_bitcast_fusion.9
  60.0 2.2 %fusion.20 = f32[16,32,64,4]{2,1,3,0:T(8,128)} fusion(f32[16,32,64,4]{2,1,3,0:T(8,128)} %get-tuple-element.168, s32[]{:T(128)} %get-tuple-element.167, bf16[64,3,8,512]{3,0,2,1:T(8,128)(2,1)S(1)} %get-tuple-element.179, f32[8,512]{1,0:T(8,128)S(1)} %broadcast_divide_fusion.2, f32[4,8,3,512]{3,1,0,2:T(8,128)S(1)} %get-tuple-element.153, ...), kind=kOutput, calls=%fused_computation.5.clone.1 | convolution fusion | flops 212336640 | bytes 3817984 | tf_op jit(solution)/shard_map/while/body/eval_jaxpr/ikedp,jdep->ijk/dot_general | solution.py:78
  62.1 1.1 constant_dynamic-slice_fusion.2
  63.3 0.2 slice_bitcast_fusion.9
  63.6 2.2 %fusion.20 = f32[16,32,64,4]{2,1,3,0:T(8,128)} fusion(f32[16,32,64,4]{2,1,3,0:T(8,128)} %get-tuple-element.168, s32[]{:T(128)} %get-tuple-element.167, bf16[64,3,8,512]{3,0,2,1:T(8,128)(2,1)S(1)} %get-tuple-element.179, f32[8,512]{1,0:T(8,128)S(1)} %broadcast_divide_fusion.2, f32[4,8,3,512]{3,1,0,2:T(8,128)S(1)} %get-tuple-element.153, ...), kind=kOutput, calls=%fused_computation.5.clone.1 | convolution fusion | flops 212336640 | bytes 3817984 | tf_op jit(solution)/shard_map/while/body/eval_jaxpr/ikedp,jdep->ijk/dot_general | solution.py:78
  65.8 1.1 constant_dynamic-slice_fusion.2
  67.2 2.2 %fusion.20 = f32[16,32,64,4]{2,1,3,0:T(8,128)} fusion(f32[16,32,64,4]{2,1,3,0:T(8,128)} %get-tuple-element.168, s32[]{:T(128)} %get-tuple-element.167, bf16[64,3,8,512]{3,0,2,1:T(8,128)(2,1)S(1)} %get-tuple-element.179, f32[8,512]{1,0:T(8,128)S(1)} %broadcast_divide_fusion.2, f32[4,8,3,512]{3,1,0,2:T(8,128)S(1)} %get-tuple-element.153, ...), kind=kOutput, calls=%fused_computation.5.clone.1 | convolution fusion | flops 212336640 | bytes 3817984 | tf_op jit(solution)/shard_map/while/body/eval_jaxpr/ikedp,jdep->ijk/dot_general | solution.py:78
  69.4 1.1 constant_dynamic-slice_fusion.2
  70.9 2.1 %fusion.20 = f32[16,32,64,4]{2,1,3,0:T(8,128)} fusion(f32[16,32,64,4]{2,1,3,0:T(8,128)} %get-tuple-element.168, s32[]{:T(128)} %get-tuple-element.167, bf16[64,3,8,512]{3,0,2,1:T(8,128)(2,1)S(1)} %get-tuple-element.179, f32[8,512]{1,0:T(8,128)S(1)} %broadcast_divide_fusion.2, f32[4,8,3,512]{3,1,0,2:T(8,128)S(1)} %get-tuple-element.153, ...), kind=kOutput, calls=%fused_computation.5.clone.1 | convolution fusion | flops 212336640 | bytes 3817984 | tf_op jit(solution)/shard_map/while/body/eval_jaxpr/ikedp,jdep->ijk/dot_general | solution.py:78
  73.0 1.1 constant_dynamic-slice_fusion.2
  74.2 0.2 slice_bitcast_fusion.9
  74.5 2.2 %fusion.20 = f32[16,32,64,4]{2,1,3,0:T(8,128)} fusion(f32[16,32,64,4]{2,1,3,0:T(8,128)} %get-tuple-element.168, s32[]{:T(128)} %get-tuple-element.167, bf16[64,3,8,512]{3,0,2,1:T(8,128)(2,1)S(1)} %get-tuple-element.179, f32[8,512]{1,0:T(8,128)S(1)} %broadcast_divide_fusion.2, f32[4,8,3,512]{3,1,0,2:T(8,128)S(1)} %get-tuple-element.153, ...), kind=kOutput, calls=%fused_computation.5.clone.1 | convolution fusion | flops 212336640 | bytes 3817984 | tf_op jit(solution)/shard_map/while/body/eval_jaxpr/ikedp,jdep->ijk/dot_general | solution.py:78
  76.6 1.1 constant_dynamic-slice_fusion.2
  78.1 2.2 %fusion.20 = f32[16,32,64,4]{2,1,3,0:T(8,128)} fusion(f32[16,32,64,4]{2,1,3,0:T(8,128)} %get-tuple-element.168, s32[]{:T(128)} %get-tuple-element.167, bf16[64,3,8,512]{3,0,2,1:T(8,128)(2,1)S(1)} %get-tuple-element.179, f32[8,512]{1,0:T(8,128)S(1)} %broadcast_divide_fusion.2, f32[4,8,3,512]{3,1,0,2:T(8,128)S(1)} %get-tuple-element.153, ...), kind=kOutput, calls=%fused_computation.5.clone.1 | convolution fusion | flops 212336640 | bytes 3817984 | tf_op jit(solution)/shard_map/while/body/eval_jaxpr/ikedp,jdep->ijk/dot_general | solution.py:78
  80.3 1.1 constant_dynamic-slice_fusion.2
  81.8 2.1 %fusion.20 = f32[16,32,64,4]{2,1,3,0:T(8,128)} fusion(f32[16,32,64,4]{2,1,3,0:T(8,128)} %get-tuple-element.168, s32[]{:T(128)} %get-tuple-element.167, bf16[64,3,8,512]{3,0,2,1:T(8,128)(2,1)S(1)} %get-tuple-element.179, f32[8,512]{1,0:T(8,128)S(1)} %broadcast_divide_fusion.2, f32[4,8,3,512]{3,1,0,2:T(8,128)S(1)} %get-tuple-element.153, ...), kind=kOutput, calls=%fused_computation.5.clone.1 | convolution fusion | flops 212336640 | bytes 3817984 | tf_op jit(solution)/shard_map/while/body/eval_jaxpr/ikedp,jdep->ijk/dot_general | solution.py:78
  83.9 1.1 constant_dynamic-slice_fusion.2
  85.4 2.2 %fusion.20 = f32[16,32,64,4]{2,1,3,0:T(8,128)} fusion(f32[16,32,64,4]{2,1,3,0:T(8,128)} %get-tuple-element.168, s32[]{:T(128)} %get-tuple-element.167, bf16[64,3,8,512]{3,0,2,1:T(8,128)(2,1)S(1)} %get-tuple-element.179, f32[8,512]{1,0:T(8,128)S(1)} %broadcast_divide_fusion.2, f32[4,8,3,512]{3,1,0,2:T(8,128)S(1)} %get-tuple-element.153, ...), kind=kOutput, calls=%fused_computation.5.clone.1 | convolution fusion | flops 212336640 | bytes 3817984 | tf_op jit(solution)/shard_map/while/body/eval_jaxpr/ikedp,jdep->ijk/dot_general | solution.py:78
  87.5 1.1 constant_dynamic-slice_fusion.2
  89.0 2.2 %fusion.20 = f32[16,32,64,4]{2,1,3,0:T(8,128)} fusion(f32[16,32,64,4]{2,1,3,0:T(8,128)} %get-tuple-element.168, s32[]{:T(128)} %get-tuple-element.167, bf16[64,3,8,512]{3,0,2,1:T(8,128)(2,1)S(1)} %get-tuple-element.179, f32[8,512]{1,0:T(8,128)S(1)} %broadcast_divide_fusion.2, f32[4,8,3,512]{3,1,0,2:T(8,128)S(1)} %get-tuple-element.153, ...), kind=kOutput, calls=%fused_computation.5.clone.1 | convolution fusion | flops 212336640 | bytes 3817984 | tf_op jit(solution)/shard_map/while/body/eval_jaxpr/ikedp,jdep->ijk/dot_general | solution.py:78
  91.2 1.1 constant_dynamic-slice_fusion.2
  92.6 2.2 %fusion.20 = f32[16,32,64,4]{2,1,3,0:T(8,128)} fusion(f32[16,32,64,4]{2,1,3,0:T(8,128)} %get-tuple-element.168, s32[]{:T(128)} %get-tuple-element.167, bf16[64,3,8,512]{3,0,2,1:T(8,128)(2,1)S(1)} %get-tuple-element.179, f32[8,512]{1,0:T(8,128)S(1)} %broadcast_divide_fusion.2, f32[4,8,3,512]{3,1,0,2:T(8,128)S(1)} %get-tuple-element.153, ...), kind=kOutput, calls=%fused_computation.5.clone.1 | convolution fusion | flops 212336640 | bytes 3817984 | tf_op jit(solution)/shard_map/while/body/eval_jaxpr/ikedp,jdep->ijk/dot_general | solution.py:78
  94.8 1.1 constant_dynamic-slice_fusion.2
  96.3 2.2 %fusion.20 = f32[16,32,64,4]{2,1,3,0:T(8,128)} fusion(f32[16,32,64,4]{2,1,3,0:T(8,128)} %get-tuple-element.168, s32[]{:T(128)} %get-tuple-element.167, bf16[64,3,8,512]{3,0,2,1:T(8,128)(2,1)S(1)} %get-tuple-element.179, f32[8,512]{1,0:T(8,128)S(1)} %broadcast_divide_fusion.2, f32[4,8,3,512]{3,1,0,2:T(8,128)S(1)} %get-tuple-element.153, ...), kind=kOutput, calls=%fused_computation.5.clone.1 | convolution fusion | flops 212336640 | bytes 3817984 | tf_op jit(solution)/shard_map/while/body/eval_jaxpr/ikedp,jdep->ijk/dot_general | solution.py:78
  98.4 1.1 constant_dynamic-slice_fusion.2
  99.9 2.2 %fusion.20 = f32[16,32,64,4]{2,1,3,0:T(8,128)} fusion(f32[16,32,64,4]{2,1,3,0:T(8,128)} %get-tuple-element.168, s32[]{:T(128)} %get-tuple-element.167, bf16[64,3,8,512]{3,0,2,1:T(8,128)(2,1)S(1)} %get-tuple-element.179, f32[8,512]{1,0:T(8,128)S(1)} %broadcast_divide_fusion.2, f32[4,8,3,512]{3,1,0,2:T(8,128)S(1)} %get-tuple-element.153, ...), kind=kOutput, calls=%fused_computation.5.clone.1 | convolution fusion | flops 212336640 | bytes 3817984 | tf_op jit(solution)/shard_map/while/body/eval_jaxpr/ikedp,jdep->ijk/dot_general | solution.py:78
  102.1 1.1 constant_dynamic-slice_fusion.2
  103.5 2.2 %fusion.20 = f32[16,32,64,4]{2,1,3,0:T(8,128)} fusion(f32[16,32,64,4]{2,1,3,0:T(8,128)} %get-tuple-element.168, s32[]{:T(128)} %get-tuple-element.167, bf16[64,3,8,512]{3,0,2,1:T(8,128)(2,1)S(1)} %get-tuple-element.179, f32[8,512]{1,0:T(8,128)S(1)} %broadcast_divide_fusion.2, f32[4,8,3,512]{3,1,0,2:T(8,128)S(1)} %get-tuple-element.153, ...), kind=kOutput, calls=%fused_computation.5.clone.1 | convolution fusion | flops 212336640 | bytes 3817984 | tf_op jit(solution)/shard_map/while/body/eval_jaxpr/ikedp,jdep->ijk/dot_general | solution.py:78
  105.7 1.1 constant_dynamic-slice_fusion.2
  107.2 2.2 %fusion.20 = f32[16,32,64,4]{2,1,3,0:T(8,128)} fusion(f32[16,32,64,4]{2,1,3,0:T(8,128)} %get-tuple-element.168, s32[]{:T(128)} %get-tuple-element.167, bf16[64,3,8,512]{3,0,2,1:T(8,128)(2,1)S(1)} %get-tuple-element.179, f32[8,512]{1,0:T(8,128)S(1)} %broadcast_divide_fusion.2, f32[4,8,3,512]{3,1,0,2:T(8,128)S(1)} %get-tuple-element.153, ...), kind=kOutput, calls=%fused_computation.5.clone.1 | convolution fusion | flops 212336640 | bytes 3817984 | tf_op jit(solution)/shard_map/while/body/eval_jaxpr/ikedp,jdep->ijk/dot_general | solution.py:78
  109.3 1.1 constant_dynamic-slice_fusion.2
  110.8 2.1 %fusion.20 = f32[16,32,64,4]{2,1,3,0:T(8,128)} fusion(f32[16,32,64,4]{2,1,3,0:T(8,128)} %get-tuple-element.168, s32[]{:T(128)} %get-tuple-element.167, bf16[64,3,8,512]{3,0,2,1:T(8,128)(2,1)S(1)} %get-tuple-element.179, f32[8,512]{1,0:T(8,128)S(1)} %broadcast_divide_fusion.2, f32[4,8,3,512]{3,1,0,2:T(8,128)S(1)} %get-tuple-element.153, ...), kind=kOutput, calls=%fused_computation.5.clone.1 | convolution fusion | flops 212336640 | bytes 3817984 | tf_op jit(solution)/shard_map/while/body/eval_jaxpr/ikedp,jdep->ijk/dot_general | solution.py:78
  113.0 3.1 %copy.24 = f32[32,64,64]{2,0,1:T(8,128)} copy(f32[32,64,64]{1,0,2:T(8,128)} %bitcast.5) | data formatting | bytes 1048576 | tf_op jit(solution)/shard_map/reshape | solution.py:83
  116.1 57.7 %reduce-scatter.2.cloned.1.call-done = f32[32,4,64]{2,0,1:T(8,128)} async-done(((f32[32,64,64]{2,0,1:T(8,128)}), f32[32,4,64]{2,0,1:T(8,128)}) %reduce-scatter.2.cloned.1.call-update) | async-done | bytes 32784 | tf_op jit(solution)/shard_map/reduce_scatter | solution.py:103
  173.8 0.8 broadcast_multiply_fusion
  174.7 0.7 copy.25
  (72 shorter events, 5.6 us)
Async XLA Ops:
  6.5 3.0 %copy-start.1 = (s32[8]{0:T(128)S(1)}, s32[8]{0:T(128)}, u32[]{:S(2)}) copy-start(s32[8]{0:T(128)} %param.8) | copy-start | bytes 100
  6.5 32.3 %all-gather.2.cloned.1.call-start = ((), (), s32[]{:S(2)}) async-start(), calls=%async_computation.1 | async-start | bytes 2359296 | tf_op jit(solution)/shard_map/all_gather | solution.py:92
  7.3 166.6 %reduce-scatter.2.cloned.1.call-start = ((), (), s32[]{:S(2)}) async-start(), calls=%async_computation.2 | async-start | bytes 1114112 | tf_op jit(solution)/shard_map/reduce_scatter | solution.py:103
  47.2 7.7 %copy-start = (f32[512]{0:T(512)S(1)}, f32[512]{0:T(512)}, u32[]{:S(2)}) copy-start(f32[512]{0:T(512)} %constant.23.clone) | copy-start | bytes 6148
Sparse Core Ops, SparseCore 0:
  8.9 29.9 all-gather.1
  116.2 57.5 reduce-scatter.1
where the time goes:
time: 183 us; the launch traced here: 182 us
  waiting for transfers between devices  87.6 us (48%)
  matrix products  41.2 us (23%)
  local copies, waits for them, and re-layouts  34.8 us (19%)
  between operations  13.5 us (7%)
  other arithmetic  4.61 us (3%)
    reduce_scatter x1, waiting for transfers between devices, body(): lax.psum_scatter(partial_value, 'elem', scatter_dimension=1, tiled=True)  57.7 us
    dot_general x16, matrix products, one_block(): jnp.einsum('ikedp,jdep->ijk', pairs, trial_fields, preferred_element_type...  34.5 us
    all_gather x1, waiting for transfers between devices, body(): gathered = lax.all_gather(mode_fields, 'test', axis=0, tiled=True)  29.2 us
    dynamic_slice x16, local copies, waits for them, and re-layouts, project(): result = lax.map(one_block, blocks)  17.1 us
    reshape x1, local copies, waits for them, and re-layouts, project(): grads.reshape((grad_modes // block_modes, block_modes) + grads.shape[1:])  7.71 us
    dot_general x1, matrix products, gradient(): jnp.dot(flat, table, preferred_element_type=jnp.float32)  6.71 us
  transfers between devices with their start and end apart: 2, of which 2 were waited for; matrix products, arithmetic and copies ran while one was open for 1% of the time, Pallas kernels for 0%

commit v1 on v0

--- a/solution.py
+++ b/solution.py
@@ -89,7 +89,9 @@
     point_weights = jnp.asarray(cube_weights).astype(jnp.float32)
     cube = Q**3
     total_points = mode_fields.shape[2] * lax.axis_size("elem")
-    gathered = lax.all_gather(mode_fields, "test", axis=0, tiled=True)
+    gathered = jnp.concatenate(
+        lax.all_to_all(jnp.stack([mode_fields] * lax.axis_size("test")), "test", 0, 0), axis=0
+    )
     elements = mode_fields.shape[2] // cube
     scales = element_scales(elem_type, type_scales)
     quadrature = point_weights[None, :] / jnp.prod(scales, axis=1)[:, None]

time: 183 us -> 166 us (0.907)
  local copies, waits for them, and re-layouts: 34.8 us -> 10.6 us
  other arithmetic: 4.61 us -> 22.5 us
  waiting for transfers between devices: 87.6 us -> 75.3 us
  starting transfers between devices: 0.04 us -> 4.37 us
  matrix products: 41.2 us -> 38.9 us
    all_gather x1 -> x0, waiting for transfers between devices: 29.2 us -> none  [body(): gathered = lax.all_gather(mode_fields, 'test', axis=0, tiled=True)]
    dynamic_slice x16 -> x0, local copies, waits for them, and re-layouts: 17.1 us -> none  [project(): result = lax.map(one_block, blocks)]
    all_to_all x0 -> x1, waiting for transfers between devices: none -> 17 us  [body(): lax.all_to_all(jnp.stack([mode_fields] * lax.axis_size('test')), 'test',...]
    convert_element_type x16, other arithmetic: 1.21 us -> 16.3 us  [one_block(): grad_wide = grad_block.astype(jnp.float32)]
    reshape x1 -> x0, local copies, waits for them, and re-layouts: 7.71 us -> none  [project(): grads.reshape((grad_modes // block_modes, block_modes) + grads.shape[1:])]
    all_to_all x0 -> x1, starting transfers between devices: none -> 4.37 us  [body(): lax.all_to_all(jnp.stack([mode_fields] * lax.axis_size('test')), 'test',...]
    another operation x0 -> x1, other arithmetic: none -> 2.79 us  [body(): jnp.stack([mode_fields] * lax.axis_size('test'))]
    dot_general x1, matrix products: 6.71 us -> 4.34 us  [gradient(): jnp.dot(flat, table, preferred_element_type=jnp.float32)]
  transfers between devices with their start and end apart: 2 -> 2, of which waited for: 2 -> 2; matrix products, arithmetic and copies ran while one was open for 1% -> 2% of each run, Pallas kernels for 0% -> 0%
where the time goes in v1:
time: 166 us
  waiting for transfers between devices  75.3 us (45%)
  matrix products  38.9 us (23%)
  other arithmetic  22.5 us (14%)
  between operations  13.4 us (8%)
  local copies, waits for them, and re-layouts  10.6 us (6%)
  starting transfers between devices  4.37 us (3%)
    reduce_scatter x1, waiting for transfers between devices, body(): lax.psum_scatter(partial_value, 'elem', scatter_dimension=1, tiled=True)  58.3 us
    dot_general x16, matrix products, one_block(): jnp.einsum('ikedp,jdep->ijk', pairs, trial_fields, preferred_element_type...  34.5 us
    all_to_all x1, waiting for transfers between devices, body(): lax.all_to_all(jnp.stack([mode_fields] * lax.axis_size('test')), 'test',...  17 us
    convert_element_type x16, other arithmetic, one_block(): grad_wide = grad_block.astype(jnp.float32)  16.3 us
    all_to_all x1, starting transfers between devices, body(): lax.all_to_all(jnp.stack([mode_fields] * lax.axis_size('test')), 'test',...  4.37 us
    dot_general x1, matrix products, gradient(): jnp.dot(flat, table, preferred_element_type=jnp.float32)  4.34 us
    mul x32, local copies, waits for them, and re-layouts, one_block(): summed = test_wide[:, None, 0, :, None, :] * grad_wide[None, :, 0]  3.61 us
  transfers between devices with their start and end apart: 2, of which 2 were waited for; matrix products, arithmetic and copies ran while one was open for 2% of the time, Pallas kernels for 0%

profile of v1, /device:TPU:0, one launch (start us, length us, event | category | flops | bytes accessed | tf_op | source)
XLA Modules:
  0.0 165.5 jit_solution(512550491389127668)
XLA Ops:
  6.5 2.8 %pad_maximum_fusion = bf16[2,32,3,4096]{3,1,2,0:T(8,128)(2,1)} fusion(bf16[1,32,3,4096]{3,1,2,0:T(8,128)(2,1)} %bitcast.73), kind=kLoop, calls=%fused_computation.18 | loop fusion | flops 786432 | bytes 2359296 | tf_op jit(solution)/shard_map/stack | solution.py:93
  9.3 4.4 %all-to-all-start = ((bf16[2,32,3,4096]{3,1,2,0:T(8,128)(2,1)}), bf16[2,32,3,4096]{3,1,2,0:T(8,128)(2,1)S(1)}, u32[]{:S(2)}, u32[]{:S(2)}) async-start(bf16[2,32,3,4096]{3,1,2,0:T(8,128)(2,1)} %pad_maximum_fusion), calls=%async_computation | async-start | bytes 3145728 | tf_op jit(solution)/shard_map/all_to_all | solution.py:93
  13.7 1.3 convert_element_type.34
  15.1 1.6 copy.46
  16.8 17.0 %all-to-all-done = bf16[2,32,3,4096]{3,1,2,0:T(8,128)(2,1)S(1)} async-done(((bf16[2,32,3,4096]{3,1,2,0:T(8,128)(2,1)}), bf16[2,32,3,4096]{3,1,2,0:T(8,128)(2,1)S(1)}, u32[]{:S(2)}, u32[]{:S(2)}) %all-to-all-start) | async-done | bytes 1572896 | tf_op jit(solution)/shard_map/all_to_all | solution.py:93
  34.0 0.7 copy.39
  34.7 0.5 copy.28
  35.2 0.2 copy-done.4
  35.4 4.3 %multiply_convert_fusion.6 = bf16[64,3,8,3,512]{4,2,3,1,0:T(8,128)(2,1)} fusion(f32[8,3]{0,1:T(4,128)S(1)} %multiply_reduce_fusion, bf16[3,512,512,1,1]{2,1,0,4,3:T(8,128)(2,1)S(1)} %copy-done.4, bf16[64,3,8,512,1]{3,2,0,1,4:T(8,128)(2,1)S(1)} %bitcast.70), kind=kOutput, calls=%fused_computation.16 | convolution fusion | flops 2420637696 | bytes 7864416 | tf_op jit(solution)/shard_map/dot_general | solution.py:59
  39.8 56.0 %while.11 = (s32[]{:T(128)}, f32[16,32,64,4]{2,1,3,0:T(8,128)}, f32[32,3,8,512]{3,0,2,1:T(8,128)S(1)}, bf16[16,4,3,8,3,512]{5,3,4,2,1,0:T(8,128)(2,1)}, bf16[64,...) while((s32[]{:T(128)}, f32[16,32,64,4]{2,1,3,0:T(8,128)}, ...), condition=%wide.region_3.4_spmd.clone, body=%wide.region_2.3_spmd.clone.sunk | while | flops 212488192 | bytes 9047157 | solution.py:82
  39.8 1.0 fusion.18
  41.1 2.2 %fusion.19 = f32[16,32,64,4]{2,1,3,0:T(8,128)} fusion(f32[16,32,64,4]{2,1,3,0:T(8,128)} %get-tuple-element.168, s32[]{:T(128)} %get-tuple-element.167, bf16[64,3,8,512]{3,0,2,1:T(8,128)(2,1)S(1)} %get-tuple-element.179, f32[8,512]{1,0:T(8,128)S(1)} %broadcast_divide_fusion.2, f32[4,8,3,512]{3,1,0,2:T(8,128)S(1)} %get-tuple-element.153, ...), kind=kOutput, calls=%fused_computation.5.clone.1 | convolution fusion | flops 212336640 | bytes 3817984 | tf_op jit(solution)/shard_map/while/body/eval_jaxpr/ikedp,jdep->ijk/dot_general | solution.py:78
  43.3 1.0 fusion.18
  44.3 0.2 slice_bitcast_fusion.9
  44.6 2.1 %fusion.19 = f32[16,32,64,4]{2,1,3,0:T(8,128)} fusion(f32[16,32,64,4]{2,1,3,0:T(8,128)} %get-tuple-element.168, s32[]{:T(128)} %get-tuple-element.167, bf16[64,3,8,512]{3,0,2,1:T(8,128)(2,1)S(1)} %get-tuple-element.179, f32[8,512]{1,0:T(8,128)S(1)} %broadcast_divide_fusion.2, f32[4,8,3,512]{3,1,0,2:T(8,128)S(1)} %get-tuple-element.153, ...), kind=kOutput, calls=%fused_computation.5.clone.1 | convolution fusion | flops 212336640 | bytes 3817984 | tf_op jit(solution)/shard_map/while/body/eval_jaxpr/ikedp,jdep->ijk/dot_general | solution.py:78
  46.7 1.0 fusion.18
  48.1 2.2 %fusion.19 = f32[16,32,64,4]{2,1,3,0:T(8,128)} fusion(f32[16,32,64,4]{2,1,3,0:T(8,128)} %get-tuple-element.168, s32[]{:T(128)} %get-tuple-element.167, bf16[64,3,8,512]{3,0,2,1:T(8,128)(2,1)S(1)} %get-tuple-element.179, f32[8,512]{1,0:T(8,128)S(1)} %broadcast_divide_fusion.2, f32[4,8,3,512]{3,1,0,2:T(8,128)S(1)} %get-tuple-element.153, ...), kind=kOutput, calls=%fused_computation.5.clone.1 | convolution fusion | flops 212336640 | bytes 3817984 | tf_op jit(solution)/shard_map/while/body/eval_jaxpr/ikedp,jdep->ijk/dot_general | solution.py:78
  50.2 1.0 fusion.18
  51.6 2.2 %fusion.19 = f32[16,32,64,4]{2,1,3,0:T(8,128)} fusion(f32[16,32,64,4]{2,1,3,0:T(8,128)} %get-tuple-element.168, s32[]{:T(128)} %get-tuple-element.167, bf16[64,3,8,512]{3,0,2,1:T(8,128)(2,1)S(1)} %get-tuple-element.179, f32[8,512]{1,0:T(8,128)S(1)} %broadcast_divide_fusion.2, f32[4,8,3,512]{3,1,0,2:T(8,128)S(1)} %get-tuple-element.153, ...), kind=kOutput, calls=%fused_computation.5.clone.1 | convolution fusion | flops 212336640 | bytes 3817984 | tf_op jit(solution)/shard_map/while/body/eval_jaxpr/ikedp,jdep->ijk/dot_general | solution.py:78
  53.7 1.0 fusion.18
  55.1 2.1 %fusion.19 = f32[16,32,64,4]{2,1,3,0:T(8,128)} fusion(f32[16,32,64,4]{2,1,3,0:T(8,128)} %get-tuple-element.168, s32[]{:T(128)} %get-tuple-element.167, bf16[64,3,8,512]{3,0,2,1:T(8,128)(2,1)S(1)} %get-tuple-element.179, f32[8,512]{1,0:T(8,128)S(1)} %broadcast_divide_fusion.2, f32[4,8,3,512]{3,1,0,2:T(8,128)S(1)} %get-tuple-element.153, ...), kind=kOutput, calls=%fused_computation.5.clone.1 | convolution fusion | flops 212336640 | bytes 3817984 | tf_op jit(solution)/shard_map/while/body/eval_jaxpr/ikedp,jdep->ijk/dot_general | solution.py:78
  57.2 1.0 fusion.18
  58.6 2.2 %fusion.19 = f32[16,32,64,4]{2,1,3,0:T(8,128)} fusion(f32[16,32,64,4]{2,1,3,0:T(8,128)} %get-tuple-element.168, s32[]{:T(128)} %get-tuple-element.167, bf16[64,3,8,512]{3,0,2,1:T(8,128)(2,1)S(1)} %get-tuple-element.179, f32[8,512]{1,0:T(8,128)S(1)} %broadcast_divide_fusion.2, f32[4,8,3,512]{3,1,0,2:T(8,128)S(1)} %get-tuple-element.153, ...), kind=kOutput, calls=%fused_computation.5.clone.1 | convolution fusion | flops 212336640 | bytes 3817984 | tf_op jit(solution)/shard_map/while/body/eval_jaxpr/ikedp,jdep->ijk/dot_general | solution.py:78
  60.7 1.0 fusion.18
  62.1 2.2 %fusion.19 = f32[16,32,64,4]{2,1,3,0:T(8,128)} fusion(f32[16,32,64,4]{2,1,3,0:T(8,128)} %get-tuple-element.168, s32[]{:T(128)} %get-tuple-element.167, bf16[64,3,8,512]{3,0,2,1:T(8,128)(2,1)S(1)} %get-tuple-element.179, f32[8,512]{1,0:T(8,128)S(1)} %broadcast_divide_fusion.2, f32[4,8,3,512]{3,1,0,2:T(8,128)S(1)} %get-tuple-element.153, ...), kind=kOutput, calls=%fused_computation.5.clone.1 | convolution fusion | flops 212336640 | bytes 3817984 | tf_op jit(solution)/shard_map/while/body/eval_jaxpr/ikedp,jdep->ijk/dot_general | solution.py:78
  64.2 1.0 fusion.18
  65.6 2.2 %fusion.19 = f32[16,32,64,4]{2,1,3,0:T(8,128)} fusion(f32[16,32,64,4]{2,1,3,0:T(8,128)} %get-tuple-element.168, s32[]{:T(128)} %get-tuple-element.167, bf16[64,3,8,512]{3,0,2,1:T(8,128)(2,1)S(1)} %get-tuple-element.179, f32[8,512]{1,0:T(8,128)S(1)} %broadcast_divide_fusion.2, f32[4,8,3,512]{3,1,0,2:T(8,128)S(1)} %get-tuple-element.153, ...), kind=kOutput, calls=%fused_computation.5.clone.1 | convolution fusion | flops 212336640 | bytes 3817984 | tf_op jit(solution)/shard_map/while/body/eval_jaxpr/ikedp,jdep->ijk/dot_general | solution.py:78
  67.7 1.0 fusion.18
  69.1 2.2 %fusion.19 = f32[16,32,64,4]{2,1,3,0:T(8,128)} fusion(f32[16,32,64,4]{2,1,3,0:T(8,128)} %get-tuple-element.168, s32[]{:T(128)} %get-tuple-element.167, bf16[64,3,8,512]{3,0,2,1:T(8,128)(2,1)S(1)} %get-tuple-element.179, f32[8,512]{1,0:T(8,128)S(1)} %broadcast_divide_fusion.2, f32[4,8,3,512]{3,1,0,2:T(8,128)S(1)} %get-tuple-element.153, ...), kind=kOutput, calls=%fused_computation.5.clone.1 | convolution fusion | flops 212336640 | bytes 3817984 | tf_op jit(solution)/shard_map/while/body/eval_jaxpr/ikedp,jdep->ijk/dot_general | solution.py:78
  71.2 1.0 fusion.18
  72.6 2.1 %fusion.19 = f32[16,32,64,4]{2,1,3,0:T(8,128)} fusion(f32[16,32,64,4]{2,1,3,0:T(8,128)} %get-tuple-element.168, s32[]{:T(128)} %get-tuple-element.167, bf16[64,3,8,512]{3,0,2,1:T(8,128)(2,1)S(1)} %get-tuple-element.179, f32[8,512]{1,0:T(8,128)S(1)} %broadcast_divide_fusion.2, f32[4,8,3,512]{3,1,0,2:T(8,128)S(1)} %get-tuple-element.153, ...), kind=kOutput, calls=%fused_computation.5.clone.1 | convolution fusion | flops 212336640 | bytes 3817984 | tf_op jit(solution)/shard_map/while/body/eval_jaxpr/ikedp,jdep->ijk/dot_general | solution.py:78
  74.7 1.0 fusion.18
  76.1 2.2 %fusion.19 = f32[16,32,64,4]{2,1,3,0:T(8,128)} fusion(f32[16,32,64,4]{2,1,3,0:T(8,128)} %get-tuple-element.168, s32[]{:T(128)} %get-tuple-element.167, bf16[64,3,8,512]{3,0,2,1:T(8,128)(2,1)S(1)} %get-tuple-element.179, f32[8,512]{1,0:T(8,128)S(1)} %broadcast_divide_fusion.2, f32[4,8,3,512]{3,1,0,2:T(8,128)S(1)} %get-tuple-element.153, ...), kind=kOutput, calls=%fused_computation.5.clone.1 | convolution fusion | flops 212336640 | bytes 3817984 | tf_op jit(solution)/shard_map/while/body/eval_jaxpr/ikedp,jdep->ijk/dot_general | solution.py:78
  78.2 1.0 fusion.18
  79.6 2.2 %fusion.19 = f32[16,32,64,4]{2,1,3,0:T(8,128)} fusion(f32[16,32,64,4]{2,1,3,0:T(8,128)} %get-tuple-element.168, s32[]{:T(128)} %get-tuple-element.167, bf16[64,3,8,512]{3,0,2,1:T(8,128)(2,1)S(1)} %get-tuple-element.179, f32[8,512]{1,0:T(8,128)S(1)} %broadcast_divide_fusion.2, f32[4,8,3,512]{3,1,0,2:T(8,128)S(1)} %get-tuple-element.153, ...), kind=kOutput, calls=%fused_computation.5.clone.1 | convolution fusion | flops 212336640 | bytes 3817984 | tf_op jit(solution)/shard_map/while/body/eval_jaxpr/ikedp,jdep->ijk/dot_general | solution.py:78
  81.7 1.0 fusion.18
  83.1 2.2 %fusion.19 = f32[16,32,64,4]{2,1,3,0:T(8,128)} fusion(f32[16,32,64,4]{2,1,3,0:T(8,128)} %get-tuple-element.168, s32[]{:T(128)} %get-tuple-element.167, bf16[64,3,8,512]{3,0,2,1:T(8,128)(2,1)S(1)} %get-tuple-element.179, f32[8,512]{1,0:T(8,128)S(1)} %broadcast_divide_fusion.2, f32[4,8,3,512]{3,1,0,2:T(8,128)S(1)} %get-tuple-element.153, ...), kind=kOutput, calls=%fused_computation.5.clone.1 | convolution fusion | flops 212336640 | bytes 3817984 | tf_op jit(solution)/shard_map/while/body/eval_jaxpr/ikedp,jdep->ijk/dot_general | solution.py:78
  85.2 1.0 fusion.18
  86.6 2.2 %fusion.19 = f32[16,32,64,4]{2,1,3,0:T(8,128)} fusion(f32[16,32,64,4]{2,1,3,0:T(8,128)} %get-tuple-element.168, s32[]{:T(128)} %get-tuple-element.167, bf16[64,3,8,512]{3,0,2,1:T(8,128)(2,1)S(1)} %get-tuple-element.179, f32[8,512]{1,0:T(8,128)S(1)} %broadcast_divide_fusion.2, f32[4,8,3,512]{3,1,0,2:T(8,128)S(1)} %get-tuple-element.153, ...), kind=kOutput, calls=%fused_computation.5.clone.1 | convolution fusion | flops 212336640 | bytes 3817984 | tf_op jit(solution)/shard_map/while/body/eval_jaxpr/ikedp,jdep->ijk/dot_general | solution.py:78
  88.7 1.0 fusion.18
  90.1 2.1 %fusion.19 = f32[16,32,64,4]{2,1,3,0:T(8,128)} fusion(f32[16,32,64,4]{2,1,3,0:T(8,128)} %get-tuple-element.168, s32[]{:T(128)} %get-tuple-element.167, bf16[64,3,8,512]{3,0,2,1:T(8,128)(2,1)S(1)} %get-tuple-element.179, f32[8,512]{1,0:T(8,128)S(1)} %broadcast_divide_fusion.2, f32[4,8,3,512]{3,1,0,2:T(8,128)S(1)} %get-tuple-element.153, ...), kind=kOutput, calls=%fused_computation.5.clone.1 | convolution fusion | flops 212336640 | bytes 3817984 | tf_op jit(solution)/shard_map/while/body/eval_jaxpr/ikedp,jdep->ijk/dot_general | solution.py:78
  92.2 1.0 fusion.18
  93.3 0.2 slice_bitcast_fusion.9
  93.6 2.2 %fusion.19 = f32[16,32,64,4]{2,1,3,0:T(8,128)} fusion(f32[16,32,64,4]{2,1,3,0:T(8,128)} %get-tuple-element.168, s32[]{:T(128)} %get-tuple-element.167, bf16[64,3,8,512]{3,0,2,1:T(8,128)(2,1)S(1)} %get-tuple-element.179, f32[8,512]{1,0:T(8,128)S(1)} %broadcast_divide_fusion.2, f32[4,8,3,512]{3,1,0,2:T(8,128)S(1)} %get-tuple-element.153, ...), kind=kOutput, calls=%fused_computation.5.clone.1 | convolution fusion | flops 212336640 | bytes 3817984 | tf_op jit(solution)/shard_map/while/body/eval_jaxpr/ikedp,jdep->ijk/dot_general | solution.py:78
  95.7 3.1 %copy.29 = f32[32,64,64]{2,0,1:T(8,128)} copy(f32[32,64,64]{1,0,2:T(8,128)} %bitcast.6) | data formatting | bytes 1048576 | tf_op jit(solution)/shard_map/reshape | solution.py:83
  98.9 58.3 %reduce-scatter.2.cloned.1.call-done = f32[32,4,64]{2,0,1:T(8,128)} async-done(((f32[32,64,64]{2,0,1:T(8,128)}), f32[32,4,64]{2,0,1:T(8,128)}) %reduce-scatter.2.cloned.1.call-update) | async-done | bytes 32784 | tf_op jit(solution)/shard_map/reduce_scatter | solution.py:105
  157.2 0.8 broadcast_multiply_fusion
  158.0 0.7 copy.30
  (63 shorter events, 4.8 us)
Async XLA Ops:
  6.5 7.2 %copy-start = (bf16[32,3,4096]{2,0,1:T(8,128)(2,1)S(1)}, bf16[32,3,4096]{2,0,1:T(8,128)(2,1)}, u32[]{:S(2)}) copy-start(bf16[32,3,4096]{2,0,1:T(8,128)(2,1)} %param.7) | copy-start | bytes 2359300
  9.3 5.7 %copy-start.2 = (f32[4,3]{1,0:T(4,128)S(1)}, f32[4,3]{1,0:T(4,128)}, u32[]{:S(2)}) copy-start(f32[4,3]{1,0:T(4,128)} %param.9) | copy-start | bytes 148
  9.3 24.5 %all-to-all-start = ((bf16[2,32,3,4096]{3,1,2,0:T(8,128)(2,1)}), bf16[2,32,3,4096]{3,1,2,0:T(8,128)(2,1)S(1)}, u32[]{:S(2)}, u32[]{:S(2)}) async-start(bf16[2,32,3,4096]{3,1,2,0:T(8,128)(2,1)} %pad_maximum_fusion), calls=%async_computation | async-start | bytes 3145728 | tf_op jit(solution)/shard_map/all_to_all | solution.py:93
  13.7 3.0 %copy-start.3 = (s32[8]{0:T(128)S(1)}, s32[8]{0:T(128)}, u32[]{:S(2)}) copy-start(s32[8]{0:T(128)} %param.8) | copy-start | bytes 100
  13.7 143.5 %reduce-scatter.2.cloned.1.call-start = ((), (), s32[]{:S(2)}) async-start(), calls=%async_computation.2 | async-start | bytes 1114112 | tf_op jit(solution)/shard_map/reduce_scatter | solution.py:105
  34.0 1.4 copy-start.4
  35.4 4.3 %copy-start.1 = (f32[512]{0:T(512)S(1)}, f32[512]{0:T(512)}, u32[]{:S(2)}) copy-start(f32[512]{0:T(512)} %constant.23.clone) | copy-start | bytes 6148
Sparse Core Ops, SparseCore 0:
  99.0 58.1 reduce-scatter.1
